TPU v7x, 32 devices: a whole 2x2x4 slice. The times are simulated.
32 devices in a mesh: section: 2 (over x), outer: 4 (over y, core), tensor: 4 (over z).
Axes of the slice: x: 2, y: 2, z: 4, core: 2. Of those that a mesh axis runs over, the one named last changes fastest.
Arguments:
- act_in: bfloat16 [2, 16, 8192], P('section', 'outer', 'tensor'), may hold values from -6 to 6
- saved_in: bfloat16 [2, 16, 8192], P('section', 'outer', 'tensor'), may hold values from -6 to 6
- cotangent: bfloat16 [2, 16, 8192], P('section', 'outer', 'tensor'), may hold values from -6 to 6
- w_gate: bfloat16 [2, 8192, 14336], P('section', 'tensor', 'outer'), may hold values from -0.0625 to 0.0625
- w_up: bfloat16 [2, 8192, 14336], P('section', 'tensor', 'outer'), may hold values from -0.0625 to 0.0625
- w_down: bfloat16 [2, 14336, 8192], P('section', 'outer', 'tensor'), may hold values from -0.046875 to 0.046875
Outputs:
- forward_sent: bfloat16 [2, 16, 8192], P('section', 'outer', 'tensor')
- grad_sent: bfloat16 [2, 16, 8192], P('section', 'outer', 'tensor')
All inputs are finite; a program needn't handle non-finite values.
Results may differ from a plain program's by a relative error of at most 0.025.
Values may be sent and summed in bfloat16 or wider, within the bound.
A program may use at most 128 MiB of HBM per device.

v0:
```python
import jax
import jax.numpy as jnp
from jax import lax
from jax.sharding import PartitionSpec as P


def shifted(shard, axis, by):
    size = lax.axis_size(axis)
    return lax.ppermute(shard, axis, [(i, (i + by) % size) for i in range(size)])


def reorder(matrix, groups):
    cells = matrix.shape[0] // (groups * groups)
    return (
        matrix.reshape(groups, groups, cells, matrix.shape[1])
        .transpose(1, 0, 2, 3)
        .reshape(matrix.shape)
    )


def rounded(product):
    return lax.optimization_barrier(product.astype(jnp.bfloat16)).astype(jnp.float32)


def pointwise(totals, width):
    gate_pre = totals[:, :width]
    up_pre = totals[:, width : 2 * width]
    gate_saved = totals[:, 2 * width : 3 * width]
    up_saved = totals[:, 3 * width : 4 * width]
    hidden_grad = totals[:, 4 * width :]
    hidden = (jax.nn.silu(gate_pre) * up_pre).astype(jnp.bfloat16)
    squash = jax.nn.sigmoid(gate_saved)
    gate_grad = (hidden_grad * up_saved * squash * (1.0 + gate_saved * (1.0 - squash))).astype(
        jnp.bfloat16
    )
    up_grad = (hidden_grad * gate_saved * squash).astype(jnp.bfloat16)
    return (hidden, gate_grad, up_grad)


def on_device(act_in, saved_in, cotangent, w_gate, w_up, w_down):
    current = act_in[0]
    stored = saved_in[0]
    incoming = cotangent[0]
    gate_mat = w_gate[0]
    up_mat = w_up[0]
    down_mat = w_down[0]
    width = gate_mat.shape[1]
    model_width = current.shape[1]
    groups = lax.axis_size("outer")
    own_rows = current.shape[0]
    contract = (((1,), (1,)), ((), ()))
    current_all, stored_all, incoming_all = (
        lax.all_gather(current, "outer", axis=0, tiled=True),
        lax.all_gather(stored, "outer", axis=0, tiled=True),
        lax.all_gather(incoming, "outer", axis=0, tiled=True),
    )
    products = [
        jnp.dot(current_all, gate_mat, preferred_element_type=jnp.float32),
        jnp.dot(current_all, up_mat, preferred_element_type=jnp.float32),
        jnp.dot(stored_all, gate_mat, preferred_element_type=jnp.float32),
        jnp.dot(stored_all, up_mat, preferred_element_type=jnp.float32),
        lax.dot_general(incoming_all, down_mat, contract, preferred_element_type=jnp.float32),
    ]
    totals = lax.psum(
        jnp.concatenate([rounded(product) for product in products], axis=1).astype(jnp.bfloat16),
        "tensor",
    ).astype(jnp.float32)
    hidden_all, gate_all, up_all = pointwise(totals, width)
    forward_term = jnp.dot(hidden_all, down_mat, preferred_element_type=jnp.float32)
    backward_term = lax.dot_general(
        gate_all, gate_mat, contract, preferred_element_type=jnp.float32
    )
    backward_term = backward_term + lax.dot_general(
        up_all, up_mat, contract, preferred_element_type=jnp.float32
    )
    sums = lax.psum_scatter(
        jnp.concatenate([forward_term, backward_term], axis=1).astype(jnp.bfloat16),
        "outer",
        scatter_dimension=0,
        tiled=True,
    ).astype(jnp.float32)
    output = (current.astype(jnp.float32) + sums[:, :model_width]).astype(jnp.bfloat16)
    input_grad = (incoming.astype(jnp.float32) + sums[:, model_width:]).astype(jnp.bfloat16)
    sent_out, sent_grad = shifted((output, input_grad), "section", 1)
    every_out, every_grad = (
        lax.all_gather(sent_out, "outer", axis=0, tiled=True),
        lax.all_gather(sent_grad, "outer", axis=0, tiled=True),
    )
    offset = lax.axis_index("outer") * own_rows
    sent_out = lax.dynamic_slice_in_dim(reorder(every_out, groups), offset, own_rows, 0)
    sent_grad = lax.dynamic_slice_in_dim(reorder(every_grad, groups), offset, own_rows, 0)
    return (sent_out[None], sent_grad[None])


def solution(mesh):
    return jax.shard_map(
        on_device,
        mesh=mesh,
        in_specs=(
            P("section", "outer", "tensor"),
            P("section", "outer", "tensor"),
            P("section", "outer", "tensor"),
            P("section", "tensor", "outer"),
            P("section", "tensor", "outer"),
            P("section", "outer", "tensor"),
        ),
        out_specs=(P("section", "outer", "tensor"), P("section", "outer", "tensor")),
        check_vma=False,
    )
```

profile of v0, /device:TPU:0, one launch (start us, length us, event | category | flops | bytes accessed | tf_op | source)
XLA Modules:
  0.0 172.0 jit_solution(5657813534022202592)
XLA Ops:
  7.2 0.0 all-reduce.4.cloned.1.call-start
  7.2 0.0 copy-start
  7.2 0.9 copy.15
  8.1 6.7 %all-gather = bf16[1,16,2048]{2,0,1:T(2,128)(2,1)S(1)} all-gather(bf16[1,4,2048]{2,0,1:T(2,128)(2,1)S(1)} %copy.15), channel_id=2, replica_groups=mesh['section'=2,'outer'=4,'tensor'=4] {'outer'}, dimensions={1}, use_global_device_ids=true | all-gather | bytes 81920 | tf_op jit(solution)/shard_map/all_gather | solution.py:53
  14.8 0.0 slice-start
  14.8 0.0 slice-start.1
  14.8 7.3 %fusion.16 = bf16[16,3584]{1,0:T(8,128)(2,1)S(1)} fusion(bf16[1,2048,3584]{2,1,0:T(8,128)(2,1)} %param.9, bf16[1,16,2048]{2,0,1:T(2,128)(2,1)S(1)} %all-gather), kind=kOutput, calls=%fused_computation.16 | convolution fusion | flops 234938368 | bytes 14860288 | tf_op jit(solution)/shard_map/dot_general | solution.py:58
  22.1 0.0 copy-done
  22.1 0.0 copy-start.4
  22.1 0.0 slice-start.2
  22.1 0.0 slice-start.3
  22.1 2.0 %fusion.22 = bf16[16,3584]{1,0:T(8,128)(2,1)S(1)} fusion(bf16[1,2048,3584]{2,1,0:T(8,128)(2,1)S(1)} %copy-done, bf16[1,16,2048]{2,0,1:T(2,128)(2,1)S(1)} %all-gather), kind=kOutput, calls=%fused_computation.18 | convolution fusion | flops 234938368 | bytes 14860288 | tf_op jit(solution)/shard_map/dot_general | solution.py:59
  24.1 0.0 copy-done.4
  24.2 5.6 %all-gather.1 = bf16[1,16,2048]{2,0,1:T(2,128)(2,1)S(1)} all-gather(bf16[1,4,2048]{2,0,1:T(2,128)(2,1)S(1)} %copy.16), channel_id=3, replica_groups=mesh['section'=2,'outer'=4,'tensor'=4] {'outer'}, dimensions={1}, use_global_device_ids=true | all-gather | bytes 81920 | tf_op jit(solution)/shard_map/all_gather | solution.py:54
  29.8 0.0 slice-done
  29.8 0.0 slice-done.1
  29.8 0.0 slice-done.2
  29.8 0.0 slice-done.3
  29.8 2.0 %fusion.19 = bf16[16,3584]{1,0:T(8,128)(2,1)S(1)} fusion(bf16[1,2048,3584]{2,1,0:T(8,128)(2,1)S(1)} %bitcast.72, bf16[1,16,2048]{2,0,1:T(2,128)(2,1)S(1)} %all-gather.1), kind=kOutput, calls=%fused_computation.17 | convolution fusion | flops 234938368 | bytes 14860288 | tf_op jit(solution)/shard_map/dot_general | solution.py:60
  31.8 0.0 copy-start.3
  31.8 2.0 %fusion.25 = bf16[16,3584]{1,0:T(8,128)(2,1)S(1)} fusion(bf16[1,2048,3584]{2,1,0:T(8,128)(2,1)S(1)} %copy-done, bf16[1,16,2048]{2,0,1:T(2,128)(2,1)S(1)} %all-gather.1), kind=kOutput, calls=%fused_computation.19 | convolution fusion | flops 234938368 | bytes 14860288 | tf_op jit(solution)/shard_map/dot_general | solution.py:61
  33.9 0.0 copy-done.3
  33.9 5.4 %all-gather.2 = bf16[1,16,2048]{2,0,1:T(2,128)(2,1)S(1)} all-gather(bf16[1,4,2048]{2,0,1:T(2,128)(2,1)S(1)} %copy.17), channel_id=4, replica_groups=mesh['section'=2,'outer'=4,'tensor'=4] {'outer'}, dimensions={1}, use_global_device_ids=true | all-gather | bytes 81920 | tf_op jit(solution)/shard_map/all_gather | solution.py:55
  39.3 9.1 %fusion.28 = bf16[16,3584]{1,0:T(8,128)(2,1)S(1)} fusion(bf16[1,3584,2048]{2,1,0:T(8,128)(2,1)} %param.11, bf16[1,16,2048]{2,0,1:T(2,128)(2,1)S(1)} %all-gather.2), kind=kOutput, calls=%fused_computation.20 | convolution fusion | flops 234938368 | bytes 14860288 | tf_op jit(solution)/shard_map/dot_general | solution.py:62
  48.5 0.0 copy-start.1
  48.5 0.8 copy-done.1
  49.3 0.0 all-reduce.4.cloned.1.call-update
  49.3 0.2 all-reduce.6.cloned.1.call-start
  49.5 40.5 %all-reduce.4.cloned.1.call-done = bf16[16,17920]{1,0:T(8,128)(2,1)} async-done(((bf16[16,17920]{1,0:T(8,128)(2,1)}), bf16[16,17920]{1,0:T(8,128)(2,1)}) %all-reduce.4.cloned.1.call-update) | async-done | bytes 573456 | tf_op jit(solution)/shard_map/psum | solution.py:64
  90.1 1.1 convert_element_type.55
  91.2 9.1 %fusion.4 = f32[16,2048]{1,0:T(8,128)S(1)} fusion(bf16[1,2048,3584]{2,1,0:T(8,128)(2,1)} %param.10, f32[16,17920]{1,0:T(8,128)S(1)} %convert_element_type.55), kind=kOutput, calls=%fused_computation.4 | convolution fusion | flops 235225088 | bytes 15269888 | tf_op jit(solution)/shard_map/dot_general | solution.py:73
  100.3 0.0 copy-start.5
  100.3 0.0 copy-start.2
  100.3 7.2 %fusion.37 = bf16[16,2048]{1,0:T(8,128)(2,1)S(1)} fusion(bf16[1,3584,2048]{2,1,0:T(8,128)(2,1)} %param.11, f32[16,17920]{1,0:T(8,128)S(1)} %convert_element_type.55), kind=kOutput, calls=%fused_computation.23 | convolution fusion | flops 235257856 | bytes 15204352 | tf_op jit(solution)/shard_map/dot_general | solution.py:69
  107.5 9.1 %fusion.34 = bf16[16,2048]{1,0:T(8,128)(2,1)S(1)} fusion(f32[16,2048]{1,0:T(8,128)S(1)} %fusion.4, bf16[1,2048,3584]{2,1,0:T(8,128)(2,1)} %param.9, f32[16,17920]{1,0:T(8,128)S(1)} %convert_element_type.55), kind=kOutput, calls=%fused_computation.22 | convolution fusion | flops 235520000 | bytes 15564800 | tf_op jit(solution)/shard_map/dot_general | solution.py:70
  116.6 0.7 pad_maximum_fusion
  117.3 0.0 all-reduce.6.cloned.1.call-update
  117.3 0.0 copy-done.5
  117.3 0.6 dynamic-slice
  118.5 30.6 %all-reduce.6.cloned.1.call-done = bf16[16,4096]{1,0:T(8,128)(2,1)} async-done(((bf16[16,4096]{1,0:T(8,128)(2,1)}), bf16[16,4096]{1,0:T(8,128)(2,1)}) %all-reduce.6.cloned.1.call-update) | async-done | bytes 131088
  149.1 0.9 dynamic-slice_convert_fusion
  150.0 0.0 copy-done.2
  150.0 1.5 collective-permute-start
  151.6 0.6 collective-permute-start.1
  152.1 1.7 collective-permute-done
  153.8 5.2 %all-gather.3 = bf16[4,4,2048]{2,1,0:T(4,128)(2,1)S(1)} all-gather(bf16[1,4,2048]{2,1,0:T(4,128)(2,1)S(1)} %bitcast.75), channel_id=1, replica_groups=mesh['section'=2,'outer'=4,'tensor'=4] {'outer'}, dimensions={0}, use_global_device_ids=true | all-gather | bytes 81920 | tf_op jit(solution)/shard_map/all_gather | solution.py:86
  159.1 0.1 copy.18
  159.1 0.0 collective-permute-done.1
  159.2 5.2 %all-gather.4 = bf16[4,4,2048]{2,1,0:T(4,128)(2,1)S(1)} all-gather(bf16[1,4,2048]{2,1,0:T(4,128)(2,1)S(1)} %bitcast.76), channel_id=1, replica_groups=mesh['section'=2,'outer'=4,'tensor'=4] {'outer'}, dimensions={0}, use_global_device_ids=true | all-gather | bytes 81920 | tf_op jit(solution)/shard_map/all_gather | solution.py:87
  164.4 0.1 copy.19
  164.5 0.6 dynamic-slice_bitcast_fusion
  (11 shorter events, 0.2 us)
Async XLA Ops:
  7.2 82.9 %all-reduce.4.cloned.1.call-start = ((), (), s32[]{:S(2)}) async-start(), calls=%async_computation | async-start | bytes 1146880 | tf_op jit(solution)/shard_map/psum | solution.py:64
  7.2 14.9 %copy-start = (bf16[1,2048,3584]{2,1,0:T(8,128)(2,1)S(1)}, bf16[1,2048,3584]{2,1,0:T(8,128)(2,1)}, u32[]{:S(2)}) copy-start(bf16[1,2048,3584]{2,1,0:T(8,128)(2,1)} %param.10) | copy-start | bytes 44040196
  14.8 15.0 %slice-start = ((s8[14680064]{0:T(1024)(128)(4,1)}), s8[4194304]{0:T(1024)(128)(4,1)S(1)}, s32[]{:S(2)}) async-start(s8[14680064]{0:T(1024)(128)(4,1)} %bitcast.71), calls=%async_computation.2 | async-start | bytes 8388608
  14.8 15.0 %slice-start.1 = ((s8[14680064]{0:T(1024)(128)(4,1)}), s8[4194304]{0:T(1024)(128)(4,1)S(1)}, s32[]{:S(2)}) async-start(s8[14680064]{0:T(1024)(128)(4,1)} %bitcast.71), calls=%async_computation.3 | async-start | bytes 8388608
  22.1 2.0 %copy-start.4 = (bf16[1,4,2048]{2,1,0:T(4,128)(2,1)S(1)}, bf16[1,4,2048]{2,1,0:T(4,128)(2,1)}, u32[]{:S(2)}) copy-start(bf16[1,4,2048]{2,1,0:T(4,128)(2,1)} %param.7) | copy-start | bytes 49156
  22.1 7.7 %slice-start.2 = ((s8[14680064]{0:T(1024)(128)(4,1)}), s8[4194304]{0:T(1024)(128)(4,1)S(1)}, s32[]{:S(2)}) async-start(s8[14680064]{0:T(1024)(128)(4,1)} %bitcast.71), calls=%async_computation.4 | async-start | bytes 8388608
  22.1 7.7 %slice-start.3 = ((s8[14680064]{0:T(1024)(128)(4,1)}), s8[2097152]{0:T(1024)(128)(4,1)S(1)}, s32[]{:S(2)}) async-start(s8[14680064]{0:T(1024)(128)(4,1)} %bitcast.71), calls=%async_computation.5 | async-start | bytes 4194304
  31.8 2.0 %copy-start.3 = (bf16[1,4,2048]{2,1,0:T(4,128)(2,1)S(1)}, bf16[1,4,2048]{2,1,0:T(4,128)(2,1)}, u32[]{:S(2)}) copy-start(bf16[1,4,2048]{2,1,0:T(4,128)(2,1)} %param.8) | copy-start | bytes 49156
  48.5 0.8 copy-start.1
  49.3 99.8 %all-reduce.6.cloned.1.call-start = ((), (), s32[]{:S(2)}) async-start(), calls=%async_computation.1 | async-start | bytes 262144
  100.3 17.0 %copy-start.5 = (u32[32]{0:T(128)S(1)}, u32[32]{0:T(128)}, u32[]{:S(2)}) copy-start(u32[32]{0:T(128)} %constant.23) | copy-start | bytes 388
  100.3 49.7 %copy-start.2 = (bf16[1,4,2048]{2,1,0:T(4,128)(2,1)S(1)}, bf16[1,4,2048]{2,1,0:T(4,128)(2,1)}, u32[]{:S(2)}) copy-start(bf16[1,4,2048]{2,1,0:T(4,128)(2,1)} %param.6) | copy-start | bytes 49156
  150.0 3.8 %collective-permute-start = (bf16[4,2048]{1,0:T(4,128)(2,1)S(1)}, bf16[4,2048]{1,0:T(4,128)(2,1)S(1)}, u32[]{:S(2)}, u32[]{:S(2)}) collective-permute-start(bf16[4,2048]{1,0:T(4,128)(2,1)S(1)} %get-tuple-element.3), channel_id=1, source_target_pairs={{0,16},{16,0},{1,17},{17,1},{2,18},{18,2},{3,19},{19,3},{4,20},{20... | collective-permute-start | bytes 49160 | tf_op jit(solution)/shard_map/ppermute | solution.py:9
  151.6 7.6 %collective-permute-start.1 = (bf16[4,2048]{1,0:T(4,128)(2,1)S(1)}, bf16[4,2048]{1,0:T(4,128)(2,1)S(1)}, u32[]{:S(2)}, u32[]{:S(2)}) collective-permute-start(bf16[4,2048]{1,0:T(4,128)(2,1)S(1)} %get-tuple-element.2), channel_id=1, source_target_pairs={{0,16},{16,0},{1,17},{17,1},{2,18},{18,2},{3,19},{19,3},{4,20},{20... | collective-permute-start | bytes 49160 | tf_op jit(solution)/shard_map/ppermute | solution.py:9
Sparse Core Ops, SparseCore 0:
  49.4 40.6 all-reduce.3
  117.4 31.6 all-reduce.5
where the time goes:
time: 172 us
  waiting for transfers between devices  72.9 us (42%)
  matrix products  47.8 us (28%)
  blocking collectives  28.1 us (16%)
  between operations  14.9 us (9%)
  local copies, waits for them, and re-layouts  3.27 us (2%)
  other arithmetic  2.67 us (2%)
  starting transfers between devices  2.35 us (1%)
    psum x1, waiting for transfers between devices, on_device(): lax.psum(jnp.concatenate([rounded(product) for product in products], axis...  40.5 us
    unnamed x3, waiting for transfers between devices  30.6 us
    dot_general x1, matrix products, on_device(): lax.dot_general(gate_all, gate_mat, contract, preferred_element_type=jnp....  9.09 us
    dot_general x1, matrix products, on_device(): lax.dot_general(incoming_all, down_mat, contract, preferred_element_type=...  9.06 us
    dot_general x1, matrix products, on_device(): lax.dot_general(up_all, up_mat, contract, preferred_element_type=jnp.floa...  9.05 us
    dot_general x1, matrix products, on_device(): jnp.dot(current_all, gate_mat, preferred_element_type=jnp.float32)  7.32 us
    dot_general x1, matrix products, on_device(): jnp.dot(hidden_all, down_mat, preferred_element_type=jnp.float32)  7.23 us
    all_gather x1, blocking collectives, on_device(): lax.all_gather(current, 'outer', axis=0, tiled=True)  6.67 us
  transfers between devices with their start and end apart: 4, of which 3 were waited for; matrix products, arithmetic and copies ran while one was open for 0% of the time, Pallas kernels for 0%

commit v1 on v0

v1 whole, which is shorter than its diff:
```python
import functools

import jax
import jax.numpy as jnp
from jax import lax
from jax.experimental import pallas as pl
from jax.experimental.pallas import tpu as pltpu
from jax.sharding import PartitionSpec as P

MESH = pl.DeviceIdType.MESH
F32 = jnp.float32
BF16 = jnp.bfloat16
CONTRACT_LAST = (((1,), (1,)), ((), ()))
SUM_LAG = 2
SECOND_LAG = 4


def kernel(
    sections, outers, tensors, chunks, chunk,
    act, saved, cot, w_gate, w_up, w_down,
    out_ref, grad_ref,
    gate_buf, up_buf, down_buf, gathered, staging, rows_f32, lhs_two, lhs_cot,
    products, part, arrived, shared, second_f32, total, final_out, final_in,
    load_sem, weight_sem, gather_send, gather_recv, part_send, part_recv,
    share_send, share_recv, final_send, final_recv,
):
    section = lax.axis_index("section")
    outer = lax.axis_index("outer")
    tensor = lax.axis_index("tensor")
    other = lax.rem(section + 1, sections)
    own_rows = act.shape[1]
    rows = own_rows * outers
    cells = own_rows // outers
    shard = rows // tensors

    loads = [
        pltpu.make_async_copy(source.at[0], gathered.at[which, outer], load_sem.at[which])
        for which, source in enumerate((act, saved, cot))
    ]
    for load in loads:
        load.start()

    def weight_copies(c):
        span = pl.ds(pl.multiple_of(c * chunk, chunk), chunk)
        return (
            pltpu.make_async_copy(w_gate.at[0, :, span], gate_buf.at[c], weight_sem.at[0, c]),
            pltpu.make_async_copy(w_up.at[0, :, span], up_buf.at[c], weight_sem.at[1, c]),
            pltpu.make_async_copy(w_down.at[0, span, :], down_buf.at[c], weight_sem.at[2, c]),
        )

    for c in range(chunks):
        for copy in weight_copies(c):
            copy.start()

    barrier = pltpu.get_barrier_semaphore()
    for step in range(1, outers):
        pl.semaphore_signal(
            barrier, 1, device_id={"outer": lax.rem(outer + step, outers)}, device_id_type=MESH
        )
    for step in range(1, tensors):
        pl.semaphore_signal(
            barrier, 1, device_id={"tensor": lax.rem(tensor + step, tensors)}, device_id_type=MESH
        )
    for place in range(outers):
        pl.semaphore_signal(
            barrier, 1, device_id={"section": other, "outer": place}, device_id_type=MESH
        )
    pl.semaphore_wait(barrier, 2 * outers + tensors - 2)

    def gather_copy(which, origin, target):
        return pltpu.make_async_remote_copy(
            src_ref=gathered.at[which, origin],
            dst_ref=gathered.at[which, origin],
            send_sem=gather_send.at[which, target],
            recv_sem=gather_recv.at[which, origin],
            device_id={"outer": target},
            device_id_type=MESH,
        )

    for which in range(3):
        loads[which].wait()
        for step in range(1, outers):
            gather_copy(which, outer, lax.rem(outer + step, outers)).start()

    for which in range(3):
        for step in range(1, outers):
            origin = lax.rem(outer + step, outers)
            gather_copy(which, origin, origin).wait_recv()
        for origin in range(outers):
            staging[...] = gathered[which, origin].astype(F32)
            for j in range(outers):
                to = (j * outers + origin) * cells
                rows_f32[which, to : to + cells, :] = staging[j * cells : (j + 1) * cells, :]
    lhs_two[0:rows, :] = rows_f32[0].astype(BF16)
    lhs_two[rows : 2 * rows, :] = rows_f32[1].astype(BF16)
    lhs_cot[...] = rows_f32[2].astype(BF16)
    place = lax.broadcasted_iota(jnp.int32, total.shape[1:], 0)
    mine = lax.rem(lax.div(place, cells), outers) == outer
    total[0] = jnp.where(mine, rows_f32[0], 0.0)
    total[1] = jnp.where(mine, rows_f32[2], 0.0)

    def part_copy(c, origin, target):
        return pltpu.make_async_remote_copy(
            src_ref=part.at[c, target],
            dst_ref=arrived.at[c, origin],
            send_sem=part_send.at[c, target],
            recv_sem=part_recv.at[c, origin],
            device_id={"tensor": target},
            device_id_type=MESH,
        )

    def share_copy(c, origin, target):
        return pltpu.make_async_remote_copy(
            src_ref=shared.at[c, origin],
            dst_ref=shared.at[c, origin],
            send_sem=share_send.at[c, target],
            recv_sem=share_recv.at[c, origin],
            device_id={"tensor": target},
            device_id_type=MESH,
        )

    def first(c):
        for copy in weight_copies(c):
            copy.wait()
        two = lhs_two[...]
        products[0 : 2 * rows, :] = jnp.dot(two, gate_buf[c], preferred_element_type=F32)
        products[2 * rows : 4 * rows, :] = jnp.dot(two, up_buf[c], preferred_element_type=F32)
        products[4 * rows : 5 * rows, :] = lax.dot_general(
            lhs_cot[...], down_buf[c], CONTRACT_LAST, preferred_element_type=F32
        )
        for target in range(tensors):
            for which in range(5):
                part[c, target, which] = products[
                    which * rows + target * shard : which * rows + (target + 1) * shard, :
                ].astype(BF16)
        for step in range(1, tensors):
            part_copy(c, tensor, lax.rem(tensor + step, tensors)).start()

    def combine(c):
        for step in range(1, tensors):
            origin = lax.rem(tensor + step, tensors)
            part_copy(c, origin, origin).wait_recv()
        sums = []
        for which in range(5):
            summed = part[c, tensor, which].astype(F32)
            for step in range(1, tensors):
                summed = summed + arrived[c, lax.rem(tensor + step, tensors), which].astype(F32)
            sums.append(summed)
        gate_pre, gate_saved, up_pre, up_saved, hidden_grad = sums
        squash = jax.nn.sigmoid(gate_saved)
        shared[c, tensor, 0] = (gate_pre * jax.nn.sigmoid(gate_pre) * up_pre).astype(BF16)
        shared[c, tensor, 1] = (
            hidden_grad * up_saved * squash * (1.0 + gate_saved * (1.0 - squash))
        ).astype(BF16)
        shared[c, tensor, 2] = (hidden_grad * gate_saved * squash).astype(BF16)
        for step in range(1, tensors):
            share_copy(c, tensor, lax.rem(tensor + step, tensors)).start()

    def second(c):
        for step in range(1, tensors):
            origin = lax.rem(tensor + step, tensors)
            share_copy(c, origin, origin).wait_recv()
        for origin in range(tensors):
            for which in range(3):
                second_f32[which, origin * shard : (origin + 1) * shard, :] = shared[
                    c, origin, which
                ].astype(F32)
        total[0] += jnp.dot(
            second_f32[0].astype(BF16), down_buf[c], preferred_element_type=F32
        )
        total[1] += lax.dot_general(
            second_f32[1].astype(BF16), gate_buf[c], CONTRACT_LAST, preferred_element_type=F32
        ) + lax.dot_general(
            second_f32[2].astype(BF16), up_buf[c], CONTRACT_LAST, preferred_element_type=F32
        )

    def advance(step, carry):
        @pl.when(step < chunks)
        def _():
            first(step)

        @pl.when((step >= SUM_LAG) & (step < chunks + SUM_LAG))
        def _():
            combine(step - SUM_LAG)

        @pl.when(step >= SECOND_LAG)
        def _():
            second(step - SECOND_LAG)

        return carry

    lax.fori_loop(0, chunks + SECOND_LAG, advance, 0)

    def final_copy(origin, target):
        return pltpu.make_async_remote_copy(
            src_ref=final_out.at[target],
            dst_ref=final_in.at[origin],
            send_sem=final_send.at[target],
            recv_sem=final_recv.at[origin],
            device_id={"section": other, "outer": target},
            device_id_type=MESH,
        )

    for target in range(outers):
        for which in range(2):
            final_out[target, which] = total[
                which, target * own_rows : (target + 1) * own_rows, :
            ].astype(BF16)
        final_copy(outer, target).start()

    def drain(c, carry):
        for step in range(1, tensors):
            target = lax.rem(tensor + step, tensors)
            part_copy(c, tensor, target).wait_send()
            share_copy(c, tensor, target).wait_send()
        return carry

    lax.fori_loop(0, chunks, drain, 0)
    for which in range(3):
        for step in range(1, outers):
            gather_copy(which, outer, lax.rem(outer + step, outers)).wait_send()

    for origin in range(outers):
        final_copy(origin, origin).wait_recv()
    for which, result in enumerate((out_ref, grad_ref)):
        summed = final_in[0, which].astype(F32)
        for origin in range(1, outers):
            summed = summed + final_in[origin, which].astype(F32)
        result[0] = summed.astype(BF16)
    for target in range(outers):
        final_copy(outer, target).wait_send()


def solution(mesh):
    sections, outers, tensors = (mesh.shape[name] for name in ("section", "outer", "tensor"))

    def on_device(act_in, saved_in, cotangent, w_gate, w_up, w_down):
        own_rows, model_width = act_in.shape[1:]
        width = w_gate.shape[2]
        rows = own_rows * outers
        shard = rows // tensors
        chunk = next(size for size in (512, 256, 128, width) if width % size == 0)
        chunks = width // chunk
        dma = pltpu.SemaphoreType.DMA
        out = jax.ShapeDtypeStruct((1, own_rows, model_width), BF16)
        return pl.pallas_call(
            functools.partial(kernel, sections, outers, tensors, chunks, chunk),
            out_shape=(out, out),
            in_specs=[pl.BlockSpec(memory_space=pl.ANY)] * 6,
            out_specs=[pl.BlockSpec(memory_space=pltpu.VMEM)] * 2,
            scratch_shapes=[
                pltpu.VMEM((chunks, model_width, chunk), BF16),
                pltpu.VMEM((chunks, model_width, chunk), BF16),
                pltpu.VMEM((chunks, chunk, model_width), BF16),
                pltpu.VMEM((3, outers, own_rows, model_width), BF16),
                pltpu.VMEM((own_rows, model_width), F32),
                pltpu.VMEM((3, rows, model_width), F32),
                pltpu.VMEM((2 * rows, model_width), BF16),
                pltpu.VMEM((rows, model_width), BF16),
                pltpu.VMEM((5 * rows, chunk), F32),
                pltpu.VMEM((chunks, tensors, 5, shard, chunk), BF16),
                pltpu.VMEM((chunks, tensors, 5, shard, chunk), BF16),
                pltpu.VMEM((chunks, tensors, 3, shard, chunk), BF16),
                pltpu.VMEM((3, rows, chunk), F32),
                pltpu.VMEM((2, rows, model_width), F32),
                pltpu.VMEM((outers, 2, own_rows, model_width), BF16),
                pltpu.VMEM((outers, 2, own_rows, model_width), BF16),
                dma((3,)),
                dma((3, chunks)),
                dma((3, outers)),
                dma((3, outers)),
                dma((chunks, tensors)),
                dma((chunks, tensors)),
                dma((chunks, tensors)),
                dma((chunks, tensors)),
                dma((outers,)),
                dma((outers,)),
            ],
            compiler_params=pltpu.CompilerParams(
                collective_id=0, has_side_effects=True, vmem_limit_bytes=60 * 1024 * 1024
            ),
        )(act_in, saved_in, cotangent, w_gate, w_up, w_down)

    return jax.shard_map(
        on_device,
        mesh=mesh,
        in_specs=(
            P("section", "outer", "tensor"),
            P("section", "outer", "tensor"),
            P("section", "outer", "tensor"),
            P("section", "tensor", "outer"),
            P("section", "tensor", "outer"),
            P("section", "outer", "tensor"),
        ),
        out_specs=(P("section", "outer", "tensor"), P("section", "outer", "tensor")),
        check_vma=False,
    )
```

time: 172 us -> 55.3 us (0.32)
  waiting for transfers between devices: 72.9 us -> 0 us
  Pallas kernels: 0 us -> 51.6 us
  matrix products: 47.8 us -> 0 us
  blocking collectives: 28.1 us -> 0 us
  between operations: 14.9 us -> 0.64 us
  other arithmetic: 2.67 us -> 0 us
  starting transfers between devices: 2.35 us -> 0 us
    pallas_call x0 -> x1, Pallas kernels: none -> 51.6 us  [on_device(): pl.pallas_call(functools.partial(kernel, sections, outers, tensors, chunk...]
    dot_general x8 -> x0, matrix products: 47.8 us -> none  [the longest x1 9.09 us: on_device(): lax.dot_general(gate_all, gate_mat, contract, preferred_element_type=jnp....]
    psum x1 -> x0, waiting for transfers between devices: 40.5 us -> none  [on_device(): lax.psum(jnp.concatenate([rounded(product) for product in products], axis...]
    unnamed x3 -> x0, waiting for transfers between devices: 30.6 us -> none
    all_gather x5 -> x0, blocking collectives: 28.1 us -> none  [the longest x1 6.67 us: on_device(): lax.all_gather(current, 'outer', axis=0, tiled=True)]
    ppermute x2 -> x0, starting transfers between devices: 2.09 us -> none  [shifted(): lax.ppermute(shard, axis, [(i, (i + by) % size) for i in range(size)])]
    convert_element_type x3 -> x0, other arithmetic: 2.01 us -> none  [the longest x1 1.13 us: on_device(): totals = lax.psum(jnp.concatenate([rounded(product) for product in produc...]
  transfers between devices with their start and end apart: 4 -> 0, of which waited for: 3 -> 0; matrix products, arithmetic and copies ran while one was open for 0% -> 0% of each run, Pallas kernels for 0% -> 0%
where the time goes in v1:
time: 55.3 us; the launch traced here: 54.9 us
  Pallas kernels  51.6 us (93%)
  local copies, waits for them, and re-layouts  2.66 us (5%)
  between operations  0.64 us (1%)
    pallas_call x1, Pallas kernels, on_device(): pl.pallas_call(functools.partial(kernel, sections, outers, tensors, chunk...  51.6 us
    unnamed x2, local copies, waits for them, and re-layouts  2.66 us

profile of v1, /device:TPU:0, one launch (start us, length us, event | category | flops | bytes accessed | tf_op | source)
XLA Modules:
  0.0 54.9 jit_solution(3250659281887020929)
XLA Ops:
  0.6 51.6 %shard_map.77 = (bf16[1,4,2048]{2,1,0:T(4,128)(2,1)}, bf16[1,4,2048]{2,1,0:T(4,128)(2,1)}) custom-call(bf16[1,4,2048]{2,1,0:T(4,128)(2,1)} %act.1, bf16[1,4,2048]{2,1,0:T(4,128)(2,1)} %saved.1, bf16[1,4,2048]{2,1,0:T(4,128)(2,1)} %cot.1, bf16[1,2048,3584]{2,1,0:T(8,128)(2,1)} %w_gate.1, bf16[1,2048,3584]{2,1,0:T(8,128)(2,1)} %w_up.1, ...), custom_call_target="tpu_custom_call" | custom-call | tf_op jit(solution)/shard_map/pallas_call | solution.py:246
  52.2 1.3 %copy.10 = bf16[1,4,2048]{2,1,0:T(4,128)(2,1)} copy(bf16[1,4,2048]{2,1,0:T(4,128)(2,1)} %get-tuple-element.4) | data formatting | bytes 32768
  53.6 1.3 %copy.11 = bf16[1,4,2048]{2,1,0:T(4,128)(2,1)} copy(bf16[1,4,2048]{2,1,0:T(4,128)(2,1)} %get-tuple-element.5) | data formatting | bytes 32768

commit v2 on v1

--- a/solution.py
+++ b/solution.py
@@ -13,6 +13,7 @@
 CONTRACT_LAST = (((1,), (1,)), ((), ()))
 SUM_LAG = 2
 SECOND_LAG = 4
+AHEAD = 2
 
 
 def kernel(
@@ -48,9 +49,9 @@
             pltpu.make_async_copy(w_down.at[0, span, :], down_buf.at[c], weight_sem.at[2, c]),
         )
 
-    for c in range(chunks):
+    for c in range(min(AHEAD, chunks)):
         for copy in weight_copies(c):
-            copy.start()
+            copy.start(priority=1)
 
     barrier = pltpu.get_barrier_semaphore()
     for step in range(1, outers):
@@ -120,6 +121,11 @@
         )
 
     def first(c):
+        @pl.when(c + AHEAD < chunks)
+        def _():
+            for copy in weight_copies(c + AHEAD):
+                copy.start(priority=1)
+
         for copy in weight_copies(c):
             copy.wait()
         two = lhs_two[...]

time: 55.3 us -> 44.9 us (0.81)
  Pallas kernels: 51.6 us -> 41.3 us
    pallas_call x1, Pallas kernels: 51.6 us -> 41.3 us  [on_device(): pl.pallas_call(functools.partial(kernel, sections, outers, tensors, chunk...]
where the time goes in v2:
time: 44.9 us; the launch traced here: 44.6 us
  Pallas kernels  41.3 us (92%)
  local copies, waits for them, and re-layouts  2.66 us (6%)
  between operations  0.64 us (1%)
    pallas_call x1, Pallas kernels, on_device(): pl.pallas_call(functools.partial(kernel, sections, outers, tensors, chunk...  41.3 us
    unnamed x2, local copies, waits for them, and re-layouts  2.66 us

profile of v2, /device:TPU:0, one launch (start us, length us, event | category | flops | bytes accessed | tf_op | source)
XLA Modules:
  0.0 44.6 jit_solution(5664619925211248216)
XLA Ops:
  0.6 41.3 %shard_map.77 = (bf16[1,4,2048]{2,1,0:T(4,128)(2,1)}, bf16[1,4,2048]{2,1,0:T(4,128)(2,1)}) custom-call(bf16[1,4,2048]{2,1,0:T(4,128)(2,1)} %act.1, bf16[1,4,2048]{2,1,0:T(4,128)(2,1)} %saved.1, bf16[1,4,2048]{2,1,0:T(4,128)(2,1)} %cot.1, bf16[1,2048,3584]{2,1,0:T(8,128)(2,1)} %w_gate.1, bf16[1,2048,3584]{2,1,0:T(8,128)(2,1)} %w_up.1, ...), custom_call_target="tpu_custom_call" | custom-call | tf_op jit(solution)/shard_map/pallas_call | solution.py:252
  41.9 1.3 %copy.10 = bf16[1,4,2048]{2,1,0:T(4,128)(2,1)} copy(bf16[1,4,2048]{2,1,0:T(4,128)(2,1)} %get-tuple-element.4) | data formatting | bytes 32768
  43.3 1.3 %copy.11 = bf16[1,4,2048]{2,1,0:T(4,128)(2,1)} copy(bf16[1,4,2048]{2,1,0:T(4,128)(2,1)} %get-tuple-element.5) | data formatting | bytes 32768
